TPU v7x, 32 devices: a whole 2x2x4 slice. The times are simulated.
32 devices in a mesh: grp: 2 (over y), row: 8 (over z, x), col: 1, ch: 2 (over core).
Axes of the slice: x: 2, y: 2, z: 4, core: 2. Of those that a mesh axis runs over, the one named last changes fastest.
Arguments:
- pair_act: bfloat16 [128, 256, 128], P('ch', ('grp', 'row'), 'col'), parts along dimension 1, may hold values from -48 to 48
- in_gain: float32 [128], P('ch'), may hold values from 0.1 to 1.9
- left_proj: bfloat16 [128, 128], P(None, 'ch'), may hold values from -0.5 to 0.5
- left_gate: bfloat16 [128, 128], P(None, 'ch'), may hold values from -0.5 to 0.5
- right_proj: bfloat16 [128, 128], P(None, 'ch'), may hold values from -0.5 to 0.5
- right_gate: bfloat16 [128, 128], P(None, 'ch'), may hold values from -0.5 to 0.5
- out_gate: bfloat16 [128, 128], P(None, 'ch'), may hold values from -0.5 to 0.5
- out_gain: float32 [128], P('ch'), may hold values from 0.1 to 1.9
- out_proj: bfloat16 [128, 128], P(None, 'ch'), may hold values from -0.5 to 0.5
Outputs:
- update: bfloat16 [128, 256, 128], P('ch', ('grp', 'row'), 'col'), parts along dimension 1
There are 2 independent parts, one for each index of `grp`. A program takes and returns all parts, laid end to end along the dimension named above; an argument that names none is the same for every part. Nothing has to cross between parts.
All inputs are finite; a program needn't handle non-finite values.
Results may differ from a plain program's by a relative error of at most 0.0085.
Values may be sent and summed in bfloat16 or wider, within the bound.
A program may use at most 64 MiB of HBM per device.

v0:
```python
import jax
import jax.numpy as jnp
from jax import lax
from jax.sharding import PartitionSpec as P


def spread_2(value, axis, source):
    kept = jnp.where(lax.axis_index(axis) == source, value, 0).astype(value.dtype)
    return lax.psum(kept, axis)


def moments(values, channel_count):
    first_sums, squares = lax.psum(
        (jnp.sum(values, axis=0), jnp.sum(values * values, axis=0)), "ch"
    )
    average = first_sums / channel_count
    spread = squares / channel_count - average * average
    centred = values - average[None]
    return centred * lax.rsqrt(spread + 1e-05)[None]


def per_device(
    pair_act, in_gain, left_proj, left_gate, right_proj, right_gate, out_gate, out_gain, out_proj
):
    row_count = pair_act.shape[1]
    col_count = pair_act.shape[2]
    hidden = left_proj.shape[1]
    fan_out = col_count // row_count
    normed = (
        moments(pair_act.astype(jnp.float32), pair_act.shape[0] * lax.axis_size("ch"))
        * in_gain[:, None, None]
    ).astype(jnp.bfloat16)
    whole = lax.all_gather(normed, "ch", axis=0, tiled=True)
    left_weights = jnp.concatenate((left_proj, left_gate), axis=1)
    left_lifted = jnp.einsum("cxy,cn->nyx", whole, left_weights, preferred_element_type=jnp.float32)
    left_edge = (jax.nn.sigmoid(left_lifted[hidden:]) * left_lifted[:hidden]).astype(jnp.bfloat16)
    other_weights = jnp.concatenate((right_proj, right_gate, out_gate), axis=1)
    other_lifted = jnp.einsum(
        "cxy,cn->nxy", whole, other_weights, preferred_element_type=jnp.float32
    )
    right_edge = (jax.nn.sigmoid(other_lifted[hidden : 2 * hidden]) * other_lifted[:hidden]).astype(
        jnp.bfloat16
    )
    gate_map = jax.nn.sigmoid(other_lifted[2 * hidden :])
    blocks = left_edge.reshape(hidden, fan_out, row_count, row_count)
    outgoing = jnp.tile(blocks, (1, lax.axis_size("row") // fan_out, 1, 1))
    arrived = lax.all_to_all(outgoing, "row", split_axis=1, concat_axis=3, tiled=True)
    left_panel = arrived.reshape(hidden, row_count, -1)
    left_panel = spread_2(left_panel, "col", lax.axis_index("row") // fan_out)
    tri_sum = jnp.einsum(
        "hik,hkj->hij",
        left_panel,
        lax.all_gather(right_edge, "row", axis=1, tiled=True),
        preferred_element_type=jnp.float32,
    )
    mid_norm = (moments(tri_sum, hidden * lax.axis_size("ch")) * out_gain[:, None, None]).astype(
        jnp.bfloat16
    )
    all_mid = lax.all_gather(mid_norm, "ch", axis=0, tiled=True)
    projected = jnp.einsum("hxy,hc->cxy", all_mid, out_proj, preferred_element_type=jnp.float32)
    return (gate_map * projected).astype(jnp.bfloat16)


def solution(mesh):
    return jax.shard_map(
        per_device,
        mesh=mesh,
        in_specs=(
            P("ch", ("grp", "row"), "col"),
            P("ch"),
            P(None, "ch"),
            P(None, "ch"),
            P(None, "ch"),
            P(None, "ch"),
            P(None, "ch"),
            P("ch"),
            P(None, "ch"),
        ),
        out_specs=P("ch", ("grp", "row"), "col"),
        check_vma=False,
    )
```

profile of v0, /device:TPU:0, one launch (start us, length us, event | category | flops | bytes accessed | tf_op | source)
XLA Modules:
  0.0 88.3 jit_solution(10436490548046105974)
XLA Ops:
  6.5 0.0 copy-start
  6.5 0.0 all-gather.2.cloned.1.call-start
  6.5 1.1 %convert_reduce_fusion = (f32[16,128]{1,0:T(8,128)S(1)}, f32[16,128]{1,0:T(8,128)S(1)}) fusion(bf16[64,16,128]{2,1,0:T(8,128)(2,1)} %param.9), kind=kLoop, calls=%fused_computation.8 | loop fusion | flops 520192 | bytes 278528 | tf_op jit(solution)/shard_map/reduce_sum | solution.py:14
  7.6 3.6 %all-reduce.1 = (f32[16,128]{1,0:T(8,128)S(1)}, f32[16,128]{1,0:T(8,128)S(1)}) all-reduce(f32[16,128]{1,0:T(8,128)S(1)} %get-tuple-element.8, f32[16,128]{1,0:T(8,128)S(1)} %get-tuple-element.7), channel_id=1, replica_groups=mesh['grp'=2,'row'=8,'col'=1,'ch'=2] {'ch'}, use_global_device_ids=true, to_apply=%region_3.0 | all-reduce | flops 4096 | bytes 32768 | tf_op jit(solution)/shard_map/psum | solution.py:13
  11.2 1.1 %fusion.6 = bf16[64,16,128]{2,0,1:T(8,128)(2,1)S(1)} fusion(f32[64]{0:T(128)} %param.10, f32[16,128]{1,0:T(8,128)S(1)} %get-tuple-element.16, f32[16,128]{1,0:T(8,128)S(1)} %get-tuple-element.15, bf16[64,16,128]{2,1,0:T(8,128)(2,1)} %param.9), kind=kLoop, calls=%fused_computation.11 | loop fusion | flops 655360 | bytes 540928 | tf_op jit(solution)/shard_map/convert_element_type | solution.py:32
  12.3 0.0 copy-start.1
  12.4 0.0 copy-start.2
  12.4 2.2 %all_gather.9 = bf16[128,16,128]{2,0,1:T(8,128)(2,1)S(1)} all-gather(bf16[64,16,128]{2,0,1:T(8,128)(2,1)S(1)} %fusion.6), channel_id=1, replica_groups=mesh['grp'=2,'row'=8,'col'=1,'ch'=2] {'ch'}, dimensions={0}, use_global_device_ids=true | all-gather | bytes 786432 | tf_op jit(solution)/shard_map/all_gather | solution.py:33
  14.5 1.1 %fusion.20 = f32[192,16,128]{2,0,1:T(8,128)S(1)} fusion(bf16[128,16,128]{2,0,1:T(8,128)(2,1)S(1)} %all_gather.9, bf16[128,64]{0,1:T(8,128)(2,1)} %param.15, bf16[128,64]{0,1:T(8,128)(2,1)} %param.14, bf16[128,64]{0,1:T(8,128)(2,1)} %param.13), kind=kOutput, calls=%fused_computation.34 | convolution fusion | flops 100810752 | bytes 2146304 | tf_op jit(solution)/shard_map/cxy,cn->nxy/dot_general | solution.py:38
  15.6 0.9 fusion.8
  16.5 0.0 all-gather.2.cloned.1.call-update
  16.5 0.0 copy-done.1
  16.6 0.0 copy-done.2
  16.6 0.3 convolution_bitcast_fusion
  16.9 0.1 fusion.12
  17.0 0.4 copy.23
  17.4 1.1 %reshape.17 = bf16[8,2,8192]{2,1,0:T(2,128)(2,1)} reshape(bf16[8,16,16,64]{3,2,1,0:T(8,128)(2,1)S(1)} %bitcast.29) | data formatting | bytes 524288
  18.5 7.0 %all-to-all-start = ((bf16[8,2,8192]{2,1,0:T(2,128)(2,1)}), bf16[8,2,8192]{2,1,0:T(2,128)(2,1)S(1)}, u32[]{:S(2)}, u32[]{:S(2)}) async-start(bf16[8,2,8192]{2,1,0:T(2,128)(2,1)} %reshape.17), calls=%async_computation | async-start | bytes 524288 | tf_op jit(solution)/shard_map/all_to_all | solution.py:47
  25.5 14.5 %all-to-all-done = bf16[8,2,8192]{2,1,0:T(2,128)(2,1)S(1)} async-done(((bf16[8,2,8192]{2,1,0:T(2,128)(2,1)}), bf16[8,2,8192]{2,1,0:T(2,128)(2,1)S(1)}, u32[]{:S(2)}, u32[]{:S(2)}) %all-to-all-start) | async-done | bytes 262176 | tf_op jit(solution)/shard_map/all_to_all | solution.py:47
  40.0 0.3 reshape.18
  40.5 0.0 copy-start.3
  40.5 0.3 copy.25
  40.8 30.4 %all-gather.2.cloned.1.call-done = bf16[64,128,128]{2,0,1:T(8,128)(2,1)} async-done(((bf16[64,16,128]{2,0,1:T(8,128)(2,1)}), bf16[64,128,128]{2,0,1:T(8,128)(2,1)}) %all-gather.2.cloned.1.call-update) | async-done | bytes 2097168 | tf_op jit(solution)/shard_map/all_gather | solution.py:53
  71.2 3.5 %fusion.30 = (f32[16,128]{1,0:T(8,128)S(1)}, f32[16,128]{1,0:T(8,128)S(1)}, f32[64,16,128]{2,1,0:T(8,128)S(1)}) fusion(bf16[64,16,128]{2,1,0:T(8,128)(2,1)S(1)} %copy.25, bf16[64,128,128]{2,0,1:T(8,128)(2,1)} %all-gather.2.cloned.1.call-done), kind=kOutput, calls=%fused_computation.49 | convolution fusion | flops 33943552 | bytes 2899968 | tf_op jit(solution)/shard_map/hik,hkj->hij/dot_general | solution.py:50
  74.6 3.3 %all-reduce = (f32[16,128]{1,0:T(8,128)S(1)}, f32[16,128]{1,0:T(8,128)S(1)}) all-reduce(f32[16,128]{1,0:T(8,128)S(1)} %get-tuple-element.6, f32[16,128]{1,0:T(8,128)S(1)} %get-tuple-element.5), channel_id=1, replica_groups=mesh['grp'=2,'row'=8,'col'=1,'ch'=2] {'ch'}, use_global_device_ids=true, to_apply=%region_7.8 | all-reduce | flops 4096 | bytes 32768 | tf_op jit(solution)/shard_map/psum | solution.py:13
  77.9 0.0 copy-done.3
  78.0 0.1 multiply_convert_fusion
  78.1 2.2 %all_gather.11 = bf16[128,16,128]{2,1,0:T(8,128)(2,1)S(1)} all-gather(bf16[64,16,128]{2,1,0:T(8,128)(2,1)S(1)} %multiply_convert_fusion), channel_id=1, replica_groups=mesh['grp'=2,'row'=8,'col'=1,'ch'=2] {'ch'}, dimensions={0}, use_global_device_ids=true | all-gather | bytes 786432 | tf_op jit(solution)/shard_map/all_gather | solution.py:59
  80.3 0.0 copy-done
  80.3 0.3 fusion.3
  80.5 0.9 copy.28
  (4 shorter events, 0.1 us)
Async XLA Ops:
  6.5 73.8 %copy-start = (bf16[128,64]{0,1:T(8,128)(2,1)S(1)}, bf16[128,64]{0,1:T(8,128)(2,1)}, u32[]{:S(2)}) copy-start(bf16[128,64]{0,1:T(8,128)(2,1)} %param.17) | copy-start | bytes 49156
  6.5 64.7 %all-gather.2.cloned.1.call-start = ((), (), s32[]{:S(2)}) async-start(), calls=%async_computation.1 | async-start | bytes 2359296 | tf_op jit(solution)/shard_map/all_gather | solution.py:53
  12.3 4.2 %copy-start.1 = (bf16[128,64]{0,1:T(8,128)(2,1)S(1)}, bf16[128,64]{0,1:T(8,128)(2,1)}, u32[]{:S(2)}) copy-start(bf16[128,64]{0,1:T(8,128)(2,1)} %param.12) | copy-start | bytes 49156
  12.4 4.2 %copy-start.2 = (bf16[128,64]{0,1:T(8,128)(2,1)S(1)}, bf16[128,64]{0,1:T(8,128)(2,1)}, u32[]{:S(2)}) copy-start(bf16[128,64]{0,1:T(8,128)(2,1)} %param.11) | copy-start | bytes 49156
  18.5 21.5 %all-to-all-start = ((bf16[8,2,8192]{2,1,0:T(2,128)(2,1)}), bf16[8,2,8192]{2,1,0:T(2,128)(2,1)S(1)}, u32[]{:S(2)}, u32[]{:S(2)}) async-start(bf16[8,2,8192]{2,1,0:T(2,128)(2,1)} %reshape.17), calls=%async_computation | async-start | bytes 524288 | tf_op jit(solution)/shard_map/all_to_all | solution.py:47
  40.5 37.5 %copy-start.3 = (f32[64]{0:T(128)S(1)}, f32[64]{0:T(128)}, u32[]{:S(2)}) copy-start(f32[64]{0:T(128)} %param.16) | copy-start | bytes 772
Sparse Core Ops, SparseCore 0:
  16.7 54.4 all-gather.1
where the time goes:
time: 88.7 us; the launch traced here: 88.3 us
  waiting for transfers between devices  45 us (51%)
  between operations  13.5 us (15%)
  blocking collectives  11.3 us (13%)
  starting transfers between devices  6.96 us (8%)
  matrix products  5.09 us (6%)
  other arithmetic  3.38 us (4%)
  local copies, waits for them, and re-layouts  3.09 us (3%)
    all_gather x1, waiting for transfers between devices, per_device(): lax.all_gather(right_edge, 'row', axis=1, tiled=True)  30.4 us
    all_to_all x1, waiting for transfers between devices, per_device(): lax.all_to_all(outgoing, 'row', split_axis=1, concat_axis=3, tiled=True)  14.5 us
    all_to_all x1, starting transfers between devices, per_device(): lax.all_to_all(outgoing, 'row', split_axis=1, concat_axis=3, tiled=True)  6.96 us
    psum x2, blocking collectives, moments(): lax.psum((jnp.sum(values, axis=0), jnp.sum(values * values, axis=0)), 'ch')  6.9 us
    dot_general x1, matrix products, per_device(): jnp.einsum('hik,hkj->hij', left_panel, lax.all_gather(right_edge, 'row',...  3.46 us
    all_gather x1, blocking collectives, per_device(): whole = lax.all_gather(normed, 'ch', axis=0, tiled=True)  2.18 us
    all_gather x1, blocking collectives, per_device(): all_mid = lax.all_gather(mid_norm, 'ch', axis=0, tiled=True)  2.18 us
  transfers between devices with their start and end apart: 2, of which 2 were waited for; matrix products, arithmetic and copies ran while one was open for 3% of the time, Pallas kernels for 0%

commit v1 on v0

--- a/solution.py
+++ b/solution.py
@@ -47,12 +47,41 @@
     arrived = lax.all_to_all(outgoing, "row", split_axis=1, concat_axis=3, tiled=True)
     left_panel = arrived.reshape(hidden, row_count, -1)
     left_panel = spread_2(left_panel, "col", lax.axis_index("row") // fan_out)
+    current_value = lax.axis_index("row")
+    x_next = lax.axis_size("row")
+    low, current_block, u1 = (x_next, current_value, right_edge.shape[1])
+    pile = [(hop_no, (hop_no + 1) % low) for hop_no in range(low)]
+    even = low // 2
+    steps_seen = [(hop_no, (hop_no - 1) % low) for hop_no in range(low)]
+    taken_in = raw_out = right_edge
     tri_sum = jnp.einsum(
         "hik,hkj->hij",
-        left_panel,
-        lax.all_gather(right_edge, "row", axis=1, tiled=True),
+        lax.dynamic_slice_in_dim(left_panel, current_block * u1, right_edge.shape[1], axis=2),
+        right_edge,
         preferred_element_type=jnp.float32,
     )
+    for q in [*range(1, even + 1)]:
+        taken_in = lax.ppermute(taken_in, axis_name="row", perm=pile)
+        if q < low - even:
+            raw_out = lax.ppermute(raw_out, "row", steps_seen)
+            extra = jnp.einsum(
+                "hik,hkj->hij",
+                lax.dynamic_slice_in_dim(
+                    left_panel, (current_block + q) % low * u1, raw_out.shape[1], axis=2
+                ),
+                raw_out,
+                preferred_element_type=jnp.float32,
+            )
+            tri_sum = tri_sum + extra
+        reached = jnp.einsum(
+            "hik,hkj->hij",
+            lax.dynamic_slice_in_dim(
+                left_panel, (current_block - q) % low * u1, taken_in.shape[1], axis=2
+            ),
+            taken_in,
+            preferred_element_type=jnp.float32,
+        )
+        tri_sum = tri_sum + reached
     mid_norm = (moments(tri_sum, hidden * lax.axis_size("ch")) * out_gain[:, None, None]).astype(
         jnp.bfloat16
     )

time: 88.7 us -> 75.7 us (0.85)
  waiting for transfers between devices: 45 us -> 24.5 us
  starting transfers between devices: 6.96 us -> 23.7 us
  between operations: 13.5 us -> 0.28 us
  local copies, waits for them, and re-layouts: 3.09 us -> 5.64 us
  matrix products: 5.09 us -> 7.22 us
    all_gather x1 -> x0, waiting for transfers between devices: 30.4 us -> none  [per_device(): lax.all_gather(right_edge, 'row', axis=1, tiled=True)]
    ppermute x0 -> x7, waiting for transfers between devices: none -> 24.5 us  [the longest x4 24.5 us: per_device(): taken_in = lax.ppermute(taken_in, axis_name='row', perm=pile)]
    ppermute x0 -> x7, starting transfers between devices: none -> 16.7 us  [the longest x4 9.49 us: per_device(): taken_in = lax.ppermute(taken_in, axis_name='row', perm=pile)]
    all_to_all x1, waiting for transfers between devices: 14.5 us -> 0.01 us  [per_device(): lax.all_to_all(outgoing, 'row', split_axis=1, concat_axis=3, tiled=True)]
    dot_general x1 -> x8, matrix products: 3.46 us -> 6.33 us  [the longest x7 6.04 us: per_device(): jnp.einsum('hik,hkj->hij', lax.dynamic_slice_in_dim(left_panel, (current_...]
    unnamed x10 -> x26, local copies, waits for them, and re-layouts: 1.46 us -> 4.2 us
  transfers between devices with their start and end apart: 2 -> 8, of which waited for: 2 -> 4; matrix products, arithmetic and copies ran while one was open for 3% -> 13% of each run, Pallas kernels for 0% -> 0%
where the time goes in v1:
time: 75.7 us; the launch traced here: 75.3 us
  waiting for transfers between devices  24.5 us (32%)
  starting transfers between devices  23.7 us (31%)
  blocking collectives  11.3 us (15%)
  matrix products  7.22 us (10%)
  local copies, waits for them, and re-layouts  5.64 us (7%)
  other arithmetic  2.68 us (4%)
    ppermute x4, waiting for transfers between devices, per_device(): taken_in = lax.ppermute(taken_in, axis_name='row', perm=pile)  24.5 us
    ppermute x4, starting transfers between devices, per_device(): taken_in = lax.ppermute(taken_in, axis_name='row', perm=pile)  9.49 us
    ppermute x3, starting transfers between devices, per_device(): raw_out = lax.ppermute(raw_out, 'row', steps_seen)  7.21 us
    all_to_all x1, starting transfers between devices, per_device(): lax.all_to_all(outgoing, 'row', split_axis=1, concat_axis=3, tiled=True)  6.96 us
    psum x2, blocking collectives, moments(): lax.psum((jnp.sum(values, axis=0), jnp.sum(values * values, axis=0)), 'ch')  6.91 us
    dot_general x7, matrix products, per_device(): jnp.einsum('hik,hkj->hij', lax.dynamic_slice_in_dim(left_panel, (current_...  6.04 us
    unnamed x26, local copies, waits for them, and re-layouts  4.2 us
    all_gather x1, blocking collectives, per_device(): whole = lax.all_gather(normed, 'ch', axis=0, tiled=True)  2.18 us
  transfers between devices with their start and end apart: 8, of which 4 were waited for; matrix products, arithmetic and copies ran while one was open for 13% of the time, Pallas kernels for 0%

profile of v1, /device:TPU:0, one launch (start us, length us, event | category | flops | bytes accessed | tf_op | source)
XLA Modules:
  0.0 75.3 jit_solution(17997379783592150171)
XLA Ops:
  0.0 1.1 %convert_reduce_fusion = (f32[16,128]{1,0:T(8,128)S(1)}, f32[16,128]{1,0:T(8,128)S(1)}) fusion(bf16[64,16,128]{2,1,0:T(8,128)(2,1)} %param.9), kind=kLoop, calls=%fused_computation.13 | loop fusion | flops 520192 | bytes 278528 | tf_op jit(solution)/shard_map/reduce_sum | solution.py:14
  1.1 3.6 %all-reduce.1 = (f32[16,128]{1,0:T(8,128)S(1)}, f32[16,128]{1,0:T(8,128)S(1)}) all-reduce(f32[16,128]{1,0:T(8,128)S(1)} %get-tuple-element.8, f32[16,128]{1,0:T(8,128)S(1)} %get-tuple-element.7), channel_id=1, replica_groups=mesh['grp'=2,'row'=8,'col'=1,'ch'=2] {'ch'}, use_global_device_ids=true, to_apply=%region_3.0 | all-reduce | flops 4096 | bytes 32768 | tf_op jit(solution)/shard_map/psum | solution.py:13
  4.7 1.1 %fusion.6 = bf16[64,16,128]{2,0,1:T(8,128)(2,1)S(1)} fusion(f32[64]{0:T(128)} %param.10, f32[16,128]{1,0:T(8,128)S(1)} %get-tuple-element.24, f32[16,128]{1,0:T(8,128)S(1)} %get-tuple-element.23, bf16[64,16,128]{2,1,0:T(8,128)(2,1)} %param.9), kind=kLoop, calls=%fused_computation.16 | loop fusion | flops 655360 | bytes 540928 | tf_op jit(solution)/shard_map/convert_element_type | solution.py:32
  5.8 2.2 %all_gather.6 = bf16[128,16,128]{2,0,1:T(8,128)(2,1)S(1)} all-gather(bf16[64,16,128]{2,0,1:T(8,128)(2,1)S(1)} %fusion.6), channel_id=1, replica_groups=mesh['grp'=2,'row'=8,'col'=1,'ch'=2] {'ch'}, dimensions={0}, use_global_device_ids=true | all-gather | bytes 786432 | tf_op jit(solution)/shard_map/all_gather | solution.py:33
  8.5 0.4 copy.44
  8.9 1.1 %reshape.17 = bf16[8,2,8192]{2,1,0:T(2,128)(2,1)} reshape(bf16[8,16,16,64]{3,2,1,0:T(8,128)(2,1)S(1)} %bitcast.36) | data formatting | bytes 524288
  10.0 7.0 %all-to-all-start = ((bf16[8,2,8192]{2,1,0:T(2,128)(2,1)}), bf16[8,2,8192]{2,1,0:T(2,128)(2,1)S(1)}, u32[]{:S(2)}, u32[]{:S(2)}) async-start(bf16[8,2,8192]{2,1,0:T(2,128)(2,1)} %reshape.17), calls=%async_computation | async-start | bytes 524288 | tf_op jit(solution)/shard_map/all_to_all | solution.py:47
  17.0 0.4 fusion.31
  17.5 2.1 %collective-permute-start.1 = (bf16[64,16,128]{2,0,1:T(8,128)(2,1)S(1)}, bf16[64,16,128]{2,0,1:T(8,128)(2,1)}, u32[]{:S(2)}, u32[]{:S(2)}) collective-permute-start(bf16[64,16,128]{2,0,1:T(8,128)(2,1)S(1)} %fusion.8), channel_id=1, source_target_pairs={{0,2},{2,4},{4,6},{6,8},{8,10},{10,12},{12,14},{14,0},{1,3},{3,5},... | collective-permute-start | bytes 786440 | tf_op jit(solution)/shard_map/ppermute | solution.py:64
  19.6 2.8 %collective-permute-start = (bf16[64,16,128]{2,0,1:T(8,128)(2,1)S(1)}, bf16[64,16,128]{2,0,1:T(8,128)(2,1)}, u32[]{:S(2)}, u32[]{:S(2)}) collective-permute-start(bf16[64,16,128]{2,0,1:T(8,128)(2,1)S(1)} %fusion.8), channel_id=1, source_target_pairs={{0,14},{2,0},{4,2},{6,4},{8,6},{10,8},{12,10},{14,12},{1,15},{3,1}... | collective-permute-start | bytes 786440 | tf_op jit(solution)/shard_map/ppermute | solution.py:66
  22.4 10.1 %collective-permute-done.1 = bf16[64,16,128]{2,0,1:T(8,128)(2,1)} collective-permute-done((bf16[64,16,128]{2,0,1:T(8,128)(2,1)S(1)}, bf16[64,16,128]{2,0,1:T(8,128)(2,1)}, u32[]{:S(2)}, u32[]{:S(2)}) %collective-permute-start.1) | collective-permute-done | bytes 262176 | tf_op jit(solution)/shard_map/ppermute | solution.py:64
  32.5 2.6 %collective-permute-start.3 = (bf16[64,16,128]{2,0,1:T(8,128)(2,1)}, bf16[64,16,128]{2,0,1:T(8,128)(2,1)}, u32[]{:S(2)}, u32[]{:S(2)}) collective-permute-start(bf16[64,16,128]{2,0,1:T(8,128)(2,1)} %collective-permute-done.1), channel_id=1, source_target_pairs={{0,2},{2,4},{4,6},{6,8},{8,10},{10,12},{12,14},{14,0},{1,3},{3,5},... | collective-permute-start | bytes 786440 | tf_op jit(solution)/shard_map/ppermute | solution.py:64
  35.1 2.1 %collective-permute-start.2 = (bf16[64,16,128]{2,0,1:T(8,128)(2,1)}, bf16[64,16,128]{2,0,1:T(8,128)(2,1)}, u32[]{:S(2)}, u32[]{:S(2)}) collective-permute-start(bf16[64,16,128]{2,0,1:T(8,128)(2,1)} %collective-permute-done), channel_id=1, source_target_pairs={{0,14},{2,0},{4,2},{6,4},{8,6},{10,8},{12,10},{14,12},{1,15},{3,1}... | collective-permute-start | bytes 786440 | tf_op jit(solution)/shard_map/ppermute | solution.py:66
  37.2 0.3 reshape.18
  38.0 0.3 fusion.29
  38.9 1.3 %convolution_add_fusion.4 = f32[64,16,128]{2,1,0:T(8,128)S(1)} fusion(f32[64,16,128]{2,1,0:T(8,128)S(1)} %fusion.29, bf16[64,16,16]{2,1,0:T(8,128)(2,1)S(1)} %copy.65, bf16[64,16,128]{2,0,1:T(8,128)(2,1)} %collective-permute-done), kind=kOutput, calls=%fused_computation.9 | convolution fusion | flops 4325376 | bytes 1343488 | tf_op jit(solution)/shard_map/hik,hkj->hij/dot_general | solution.py:67
  40.1 1.3 %convolution_add_fusion.3 = f32[64,16,128]{2,1,0:T(8,128)S(1)} fusion(f32[64,16,128]{2,1,0:T(8,128)S(1)} %convolution_add_fusion.4, bf16[64,16,16]{2,1,0:T(8,128)(2,1)S(1)} %copy.66, bf16[64,16,128]{2,0,1:T(8,128)(2,1)} %collective-permute-done.1), kind=kOutput, calls=%fused_computation.8 | convolution fusion | flops 4325376 | bytes 1343488 | tf_op jit(solution)/shard_map/hik,hkj->hij/dot_general | solution.py:76
  42.2 0.9 %copy.69 = bf16[64,16,16]{2,1,0:T(8,128)(2,1)} copy(bf16[64,16,16]{0,2,1:T(8,128)(2,1)S(1)} %get-tuple-element.15) | data formatting | bytes 65536
  43.4 2.9 %collective-permute-done.3 = bf16[64,16,128]{2,0,1:T(8,128)(2,1)} collective-permute-done((bf16[64,16,128]{2,0,1:T(8,128)(2,1)}, bf16[64,16,128]{2,0,1:T(8,128)(2,1)}, u32[]{:S(2)}, u32[]{:S(2)}) %collective-permute-start.3) | collective-permute-done | bytes 262176 | tf_op jit(solution)/shard_map/ppermute | solution.py:64
  46.2 2.5 %collective-permute-start.5 = (bf16[64,16,128]{2,0,1:T(8,128)(2,1)}, bf16[64,16,128]{2,0,1:T(8,128)(2,1)S(1)}, u32[]{:S(2)}, u32[]{:S(2)}) collective-permute-start(bf16[64,16,128]{2,0,1:T(8,128)(2,1)} %collective-permute-done.3), channel_id=1, source_target_pairs={{0,2},{2,4},{4,6},{6,8},{8,10},{10,12},{12,14},{14,0},{1,3},{3,5},... | collective-permute-start | bytes 786440 | tf_op jit(solution)/shard_map/ppermute | solution.py:64
  48.7 1.3 %fusion.24 = f32[64,16,128]{2,1,0:T(8,128)S(1)} fusion(bf16[64,16,16]{2,1,0:T(8,128)(2,1)S(1)} %copy.68, bf16[64,16,128]{2,0,1:T(8,128)(2,1)} %collective-permute-done.3), kind=kOutput, calls=%fused_computation.42 | convolution fusion | flops 4194304 | bytes 819200 | tf_op jit(solution)/shard_map/hik,hkj->hij/dot_general | solution.py:76
  50.0 2.3 %collective-permute-start.4 = (bf16[64,16,128]{2,0,1:T(8,128)(2,1)}, bf16[64,16,128]{2,0,1:T(8,128)(2,1)S(1)}, u32[]{:S(2)}, u32[]{:S(2)}) collective-permute-start(bf16[64,16,128]{2,0,1:T(8,128)(2,1)} %collective-permute-done.2), channel_id=1, source_target_pairs={{0,14},{2,0},{4,2},{6,4},{8,6},{10,8},{12,10},{14,12},{1,15},{3,1}... | collective-permute-start | bytes 786440 | tf_op jit(solution)/shard_map/ppermute | solution.py:66
  52.3 1.3 %fusion.2 = f32[64,16,128]{2,1,0:T(8,128)S(1)} fusion(f32[64,16,128]{2,1,0:T(8,128)S(1)} %fusion.24, f32[64,16,128]{2,1,0:T(8,128)S(1)} %convolution_add_fusion.3, bf16[64,16,16]{2,1,0:T(8,128)(2,1)S(1)} %copy.67, bf16[64,16,128]{2,0,1:T(8,128)(2,1)} %collective-permute-done.2), kind=kOutput, calls=%fused_computation.7 | convolution fusion | flops 4456448 | bytes 1867776 | tf_op jit(solution)/shard_map/hik,hkj->hij/dot_general | solution.py:67
  53.6 5.5 %collective-permute-done.5 = bf16[64,16,128]{2,0,1:T(8,128)(2,1)S(1)} collective-permute-done((bf16[64,16,128]{2,0,1:T(8,128)(2,1)}, bf16[64,16,128]{2,0,1:T(8,128)(2,1)S(1)}, u32[]{:S(2)}, u32[]{:S(2)}) %collective-permute-start.5) | collective-permute-done | bytes 262176 | tf_op jit(solution)/shard_map/ppermute | solution.py:64
  59.1 2.4 %collective-permute-start.6 = (bf16[64,16,128]{2,0,1:T(8,128)(2,1)S(1)}, bf16[64,16,128]{2,0,1:T(8,128)(2,1)S(1)}, u32[]{:S(2)}, u32[]{:S(2)}) collective-permute-start(bf16[64,16,128]{2,0,1:T(8,128)(2,1)S(1)} %collective-permute-done.5), channel_id=1, source_target_pairs={{0,2},{2,4},{4,6},{6,8},{8,10},{10,12},{12,14},{14,0},{1,3},{3,5},... | collective-permute-start | bytes 786440 | tf_op jit(solution)/shard_map/ppermute | solution.py:64
  61.5 0.3 fusion.21
  61.8 0.3 fusion.1
  62.1 6.0 %collective-permute-done.6 = bf16[64,16,128]{2,0,1:T(8,128)(2,1)S(1)} collective-permute-done((bf16[64,16,128]{2,0,1:T(8,128)(2,1)S(1)}, bf16[64,16,128]{2,0,1:T(8,128)(2,1)S(1)}, u32[]{:S(2)}, u32[]{:S(2)}) %collective-permute-start.6) | collective-permute-done | bytes 262176 | tf_op jit(solution)/shard_map/ppermute | solution.py:64
  68.1 0.3 fusion.41
  68.5 3.3 %all-reduce = (f32[16,128]{1,0:T(8,128)S(1)}, f32[16,128]{1,0:T(8,128)S(1)}) all-reduce(f32[16,128]{1,0:T(8,128)S(1)} %get-tuple-element.6, f32[16,128]{1,0:T(8,128)S(1)} %get-tuple-element.5), channel_id=1, replica_groups=mesh['grp'=2,'row'=8,'col'=1,'ch'=2] {'ch'}, use_global_device_ids=true, to_apply=%region_7.8 | all-reduce | flops 4096 | bytes 32768 | tf_op jit(solution)/shard_map/psum | solution.py:13
  71.9 2.2 %all_gather.7 = bf16[128,16,128]{2,1,0:T(8,128)(2,1)S(1)} all-gather(bf16[64,16,128]{2,1,0:T(8,128)(2,1)S(1)} %multiply_convert_fusion), channel_id=1, replica_groups=mesh['grp'=2,'row'=8,'col'=1,'ch'=2] {'ch'}, dimensions={0}, use_global_device_ids=true | all-gather | bytes 786432 | tf_op jit(solution)/shard_map/all_gather | solution.py:88
  74.4 0.9 %copy.63 = bf16[64,16,128]{2,1,0:T(8,128)(2,1)} copy(bf16[64,16,128]{2,0,1:T(8,128)(2,1)S(1)} %fusion.3) | data formatting | bytes 524288 | tf_op jit(solution)/shard_map/convert_element_type | solution.py:90
  (37 shorter events, 3.0 us)
Async XLA Ops:
  0.0 74.1 %copy-start = (bf16[128,64]{0,1:T(8,128)(2,1)S(1)}, bf16[128,64]{0,1:T(8,128)(2,1)}, u32[]{:S(2)}) copy-start(bf16[128,64]{0,1:T(8,128)(2,1)} %param.17) | copy-start | bytes 49156
  0.0 8.0 %copy-start.3 = (bf16[128,64]{0,1:T(8,128)(2,1)S(1)}, bf16[128,64]{0,1:T(8,128)(2,1)}, u32[]{:S(2)}) copy-start(bf16[128,64]{0,1:T(8,128)(2,1)} %param.11) | copy-start | bytes 49156
  0.0 8.0 %copy-start.2 = (bf16[128,64]{0,1:T(8,128)(2,1)S(1)}, bf16[128,64]{0,1:T(8,128)(2,1)}, u32[]{:S(2)}) copy-start(bf16[128,64]{0,1:T(8,128)(2,1)} %param.12) | copy-start | bytes 49156
  8.3 8.7 %copy-start.4 = (bf16[128,64]{0,1:T(8,128)(2,1)S(1)}, bf16[128,64]{0,1:T(8,128)(2,1)}, u32[]{:S(2)}) copy-start(bf16[128,64]{0,1:T(8,128)(2,1)} %param.15) | copy-start | bytes 49156
  8.3 8.7 %copy-start.5 = (bf16[128,64]{0,1:T(8,128)(2,1)S(1)}, bf16[128,64]{0,1:T(8,128)(2,1)}, u32[]{:S(2)}) copy-start(bf16[128,64]{0,1:T(8,128)(2,1)} %param.14) | copy-start | bytes 49156
  8.3 8.7 %copy-start.6 = (bf16[128,64]{0,1:T(8,128)(2,1)S(1)}, bf16[128,64]{0,1:T(8,128)(2,1)}, u32[]{:S(2)}) copy-start(bf16[128,64]{0,1:T(8,128)(2,1)} %param.13) | copy-start | bytes 49156
  10.0 27.2 %all-to-all-start = ((bf16[8,2,8192]{2,1,0:T(2,128)(2,1)}), bf16[8,2,8192]{2,1,0:T(2,128)(2,1)S(1)}, u32[]{:S(2)}, u32[]{:S(2)}) async-start(bf16[8,2,8192]{2,1,0:T(2,128)(2,1)} %reshape.17), calls=%async_computation | async-start | bytes 524288 | tf_op jit(solution)/shard_map/all_to_all | solution.py:47
  17.5 15.0 %collective-permute-start.1 = (bf16[64,16,128]{2,0,1:T(8,128)(2,1)S(1)}, bf16[64,16,128]{2,0,1:T(8,128)(2,1)}, u32[]{:S(2)}, u32[]{:S(2)}) collective-permute-start(bf16[64,16,128]{2,0,1:T(8,128)(2,1)S(1)} %fusion.8), channel_id=1, source_target_pairs={{0,2},{2,4},{4,6},{6,8},{8,10},{10,12},{12,14},{14,0},{1,3},{3,5},... | collective-permute-start | bytes 786440 | tf_op jit(solution)/shard_map/ppermute | solution.py:64
  19.6 15.5 %collective-permute-start = (bf16[64,16,128]{2,0,1:T(8,128)(2,1)S(1)}, bf16[64,16,128]{2,0,1:T(8,128)(2,1)}, u32[]{:S(2)}, u32[]{:S(2)}) collective-permute-start(bf16[64,16,128]{2,0,1:T(8,128)(2,1)S(1)} %fusion.8), channel_id=1, source_target_pairs={{0,14},{2,0},{4,2},{6,4},{8,6},{10,8},{12,10},{14,12},{1,15},{3,1}... | collective-permute-start | bytes 786440 | tf_op jit(solution)/shard_map/ppermute | solution.py:66
  32.5 13.7 %collective-permute-start.3 = (bf16[64,16,128]{2,0,1:T(8,128)(2,1)}, bf16[64,16,128]{2,0,1:T(8,128)(2,1)}, u32[]{:S(2)}, u32[]{:S(2)}) collective-permute-start(bf16[64,16,128]{2,0,1:T(8,128)(2,1)} %collective-permute-done.1), channel_id=1, source_target_pairs={{0,2},{2,4},{4,6},{6,8},{8,10},{10,12},{12,14},{14,0},{1,3},{3,5},... | collective-permute-start | bytes 786440 | tf_op jit(solution)/shard_map/ppermute | solution.py:64
  35.1 14.9 %collective-permute-start.2 = (bf16[64,16,128]{2,0,1:T(8,128)(2,1)}, bf16[64,16,128]{2,0,1:T(8,128)(2,1)}, u32[]{:S(2)}, u32[]{:S(2)}) collective-permute-start(bf16[64,16,128]{2,0,1:T(8,128)(2,1)} %collective-permute-done), channel_id=1, source_target_pairs={{0,14},{2,0},{4,2},{6,4},{8,6},{10,8},{12,10},{14,12},{1,15},{3,1}... | collective-permute-start | bytes 786440 | tf_op jit(solution)/shard_map/ppermute | solution.py:66
  46.2 12.9 %collective-permute-start.5 = (bf16[64,16,128]{2,0,1:T(8,128)(2,1)}, bf16[64,16,128]{2,0,1:T(8,128)(2,1)S(1)}, u32[]{:S(2)}, u32[]{:S(2)}) collective-permute-start(bf16[64,16,128]{2,0,1:T(8,128)(2,1)} %collective-permute-done.3), channel_id=1, source_target_pairs={{0,2},{2,4},{4,6},{6,8},{8,10},{10,12},{12,14},{14,0},{1,3},{3,5},... | collective-permute-start | bytes 786440 | tf_op jit(solution)/shard_map/ppermute | solution.py:64
  50.0 11.8 %copy-start.1 = (bf16[64,16,16]{2,1,0:T(8,128)(2,1)S(1)}, bf16[64,16,16]{2,1,0:T(8,128)(2,1)}, u32[]{:S(2)}) copy-start(bf16[64,16,16]{2,1,0:T(8,128)(2,1)} %copy.69) | copy-start | bytes 98308
  50.0 11.8 %collective-permute-start.4 = (bf16[64,16,128]{2,0,1:T(8,128)(2,1)}, bf16[64,16,128]{2,0,1:T(8,128)(2,1)S(1)}, u32[]{:S(2)}, u32[]{:S(2)}) collective-permute-start(bf16[64,16,128]{2,0,1:T(8,128)(2,1)} %collective-permute-done.2), channel_id=1, source_target_pairs={{0,14},{2,0},{4,2},{6,4},{8,6},{10,8},{12,10},{14,12},{1,15},{3,1}... | collective-permute-start | bytes 786440 | tf_op jit(solution)/shard_map/ppermute | solution.py:66
  59.1 9.1 %collective-permute-start.6 = (bf16[64,16,128]{2,0,1:T(8,128)(2,1)S(1)}, bf16[64,16,128]{2,0,1:T(8,128)(2,1)S(1)}, u32[]{:S(2)}, u32[]{:S(2)}) collective-permute-start(bf16[64,16,128]{2,0,1:T(8,128)(2,1)S(1)} %collective-permute-done.5), channel_id=1, source_target_pairs={{0,2},{2,4},{4,6},{6,8},{8,10},{10,12},{12,14},{14,0},{1,3},{3,5},... | collective-permute-start | bytes 786440 | tf_op jit(solution)/shard_map/ppermute | solution.py:64
  61.8 10.0 %copy-start.7 = (f32[64]{0:T(128)S(1)}, f32[64]{0:T(128)}, u32[]{:S(2)}) copy-start(f32[64]{0:T(128)} %param.16) | copy-start | bytes 772
